TPU v7x, 32 devices: a whole 2x2x4 slice. The times are simulated.
32 devices in a mesh: dp: 8 (over z, core), tensor: 4 (over y, x).
Axes of the slice: x: 2, y: 2, z: 4, core: 2. Of those that a mesh axis runs over, the one named last changes fastest.
Arguments:
- saved_queries: bfloat16 [4096, 8192], P('dp', 'tensor'), may hold values from -200 to 200
- saved_keys: bfloat16 [4096, 1024], P('dp', 'tensor'), may hold values from -200 to 200
- saved_values: bfloat16 [4096, 1024], P('dp', 'tensor'), may hold values from -6 to 6
- out_grad: bfloat16 [4096, 8192], P(('dp', 'tensor')), may hold values from -0.59765625 to 0.59765625
- act_exponent: int32 [1], replicated, may hold values from -6 to 3
- grad_exponent: int32 [1], replicated, may hold values from -4 to 1
Outputs:
- grad_weight: float32 [8192, 8192], P('dp', 'tensor')
All inputs are finite; a program needn't handle non-finite values.
Results may differ from a plain program's by a relative error of at most 0.012.
Values may be sent and summed in bfloat16 or wider, within the bound.
A program may use at most 128 MiB of HBM per device.

v0:
```python
import jax
import jax.numpy as jnp
from jax import lax
from jax.sharding import PartitionSpec as P

HEAD_DIM = 128


SATURATION = 448.0


def quantize(values_in, exponent):
    factor = SATURATION * jnp.exp2(-exponent[0].astype(jnp.float32))
    return jnp.clip(values_in * factor, -SATURATION, SATURATION).astype(jnp.bfloat16)


def attend(query_rows, key_rows, value_rows):
    scores = jnp.dot(query_rows, key_rows.T, preferred_element_type=jnp.float32) * HEAD_DIM ** (
        -0.5
    )
    positions = jnp.arange(query_rows.shape[0], dtype=jnp.int32)
    causal = positions[None, :] <= positions[:, None]
    scores = jnp.where(causal, scores, jnp.float32(-1e30))
    row_max = jnp.max(scores, axis=1, keepdims=True)
    weights = jnp.exp(scores - row_max)
    probabilities = (weights / jnp.sum(weights, axis=1, keepdims=True)).astype(jnp.bfloat16)
    return jnp.dot(probabilities, value_rows, preferred_element_type=jnp.float32)


def on_device(saved_queries, saved_keys, saved_values, out_grad, act_exponent, grad_exponent):
    seq_len = saved_queries.shape[0]
    local_width = saved_queries.shape[1]
    heads_here = local_width // HEAD_DIM
    per_group = heads_here // (saved_keys.shape[1] // HEAD_DIM)
    dequant = jnp.exp2((act_exponent[0] + grad_exponent[0]).astype(jnp.float32)) / (
        SATURATION * SATURATION
    )

    def one_head(head_index, scaled_rows):
        query_rows = lax.dynamic_slice_in_dim(saved_queries, head_index * HEAD_DIM, HEAD_DIM, 1)
        kv_start = head_index // per_group * HEAD_DIM
        key_rows = lax.dynamic_slice_in_dim(saved_keys, kv_start, HEAD_DIM, 1)
        value_rows = lax.dynamic_slice_in_dim(saved_values, kv_start, HEAD_DIM, 1)
        attended = attend(query_rows, key_rows, value_rows)
        return lax.dynamic_update_slice_in_dim(
            scaled_rows, quantize(attended, act_exponent), head_index * HEAD_DIM, 1
        )

    act_scaled = lax.fori_loop(
        0, heads_here, one_head, jnp.zeros((seq_len, local_width), jnp.bfloat16)
    )
    grad_scaled = quantize(out_grad.astype(jnp.float32), grad_exponent)
    running = lax.dot_general(
        lax.all_gather(grad_scaled, "tensor", axis=0, tiled=True),
        act_scaled,
        (((0,), (0,)), ((), ())),
        preferred_element_type=jnp.float32,
    )
    grad_weight = lax.psum_scatter(
        (running * dequant).astype(jnp.bfloat16), "dp", scatter_dimension=0, tiled=True
    ).astype(jnp.float32)
    return grad_weight


def solution(mesh):
    in_specs = (
        P("dp", "tensor"),
        P("dp", "tensor"),
        P("dp", "tensor"),
        P(("dp", "tensor"), None),
        P(),
        P(),
    )
    out_specs = P("dp", "tensor")
    return jax.shard_map(
        on_device, mesh=mesh, in_specs=in_specs, out_specs=out_specs, check_vma=False
    )
```

profile of v0, /device:TPU:0, one launch (start us, length us, event | category | flops | bytes accessed | tf_op | source)
XLA Modules:
  0.0 465.3 jit_solution(4609966031278577632)
XLA Ops:
  6.5 0.0 all-gather.2.cloned.1.call-start
  7.2 0.0 copy-start
  7.2 0.0 copy-start.1
  7.3 3.5 clamp_convert_fusion
  10.7 0.0 all-gather.2.cloned.1.call-update
  10.8 0.0 reduce-scatter.2.cloned.1.call-start
  11.6 0.2 broadcast_in_dim.26
  11.8 0.0 copy-done
  11.8 0.0 copy-done.1
  11.8 30.4 %while.15 = (s32[]{:T(128)}, bf16[512,2048]{1,0:T(8,128)(2,1)S(1)}, bf16[512,2048]{1,0:T(8,128)(2,1)}, bf16[512,256]{1,0:T(8,128)(2,1)S(1)}, bf16[512,256]{1,0:T...) while((s32[]{:T(128)}, bf16[512,2048]{1,0:T(8,128)(2,1)S(1)}, ...), condition=%wide.region_3.4_spmd, body=%wide.region_0.3_spmd.sunk | while | flops 136772624 | bytes 3680587 | solution.py:49
  11.9 1.2 fusion.20
  13.1 0.2 fusion.21
  13.3 0.4 fusion.22
  13.8 1.2 fusion.20
  15.0 0.2 fusion.21
  15.2 0.4 fusion.22
  15.6 1.2 fusion.20
  16.9 0.2 fusion.21
  17.1 0.4 fusion.22
  17.5 1.2 fusion.20
  18.8 0.2 fusion.21
  19.0 0.4 fusion.22
  19.4 1.3 fusion.20
  20.7 0.2 fusion.21
  20.9 0.4 fusion.22
  21.4 1.3 fusion.20
  22.6 0.2 fusion.21
  22.8 0.4 fusion.22
  23.3 1.2 fusion.20
  24.5 0.2 fusion.21
  24.7 0.4 fusion.22
  25.2 1.2 fusion.20
  26.4 0.2 fusion.21
  26.6 0.4 fusion.22
  27.1 1.2 fusion.20
  28.3 0.2 fusion.21
  28.5 0.4 fusion.22
  29.0 1.2 fusion.20
  30.2 0.2 fusion.21
  30.4 0.4 fusion.22
  30.9 1.2 fusion.20
  32.1 0.2 fusion.21
  32.3 0.4 fusion.22
  32.8 1.2 fusion.20
  34.0 0.2 fusion.21
  34.2 0.4 fusion.22
  34.7 1.2 fusion.20
  35.9 0.2 fusion.21
  36.1 0.4 fusion.22
  36.6 1.2 fusion.20
  37.8 0.2 fusion.21
  38.0 0.4 fusion.22
  38.5 1.2 fusion.20
  39.7 0.2 fusion.21
  39.9 0.4 fusion.22
  40.4 1.2 fusion.20
  41.6 0.2 fusion.21
  41.8 0.4 fusion.22
  42.3 58.9 %all-gather.2.cloned.1.call-done = bf16[512,8192]{1,0:T(8,128)(2,1)} async-done(((bf16[128,8192]{1,0:T(8,128)(2,1)}), bf16[512,8192]{1,0:T(8,128)(2,1)}) %all-gather.2.cloned.1.call-update) | async-done | bytes 8388624 | tf_op jit(solution)/shard_map/all_gather | solution.py:54
  101.1 25.0 %multiply_convert_fusion = bf16[8192,2048]{1,0:T(8,128)(2,1)} fusion(bf16[512,8192]{1,0:T(8,128)(2,1)} %all-gather.2.cloned.1.call-done, bf16[512,2048]{1,0:T(8,128)(2,1)S(1)} %get-tuple-element.166, f32[]{:T(128)} %bitcast.2), kind=kOutput, calls=%fused_computation.17 | convolution fusion | flops 17213423616 | bytes 44040196 | tf_op jit(solution)/shard_map/dot_general | solution.py:53
  126.1 0.0 reduce-scatter.2.cloned.1.call-update
  126.2 325.6 %reduce-scatter.2.cloned.1.call-done = bf16[1024,2048]{1,0:T(8,128)(2,1)} async-done(((bf16[8192,2048]{1,0:T(8,128)(2,1)}), bf16[1024,2048]{1,0:T(8,128)(2,1)}) %reduce-scatter.2.cloned.1.call-update) | async-done | bytes 4194320 | tf_op jit(solution)/shard_map/reduce_scatter | solution.py:59
  451.8 6.7 %convert_element_type.56 = f32[1024,2048]{1,0:T(8,128)} convert(bf16[1024,2048]{1,0:T(8,128)(2,1)} %reduce-scatter.2.cloned.1.call-done) | non-fusion elementwise | flops 2097152 | bytes 12582912 | tf_op jit(solution)/shard_map/convert_element_type | solution.py:61
Async XLA Ops:
  6.5 94.6 %all-gather.2.cloned.1.call-start = ((), (), s32[]{:S(2)}) async-start(), calls=%async_computation.1 | async-start | bytes 10485760 | tf_op jit(solution)/shard_map/all_gather | solution.py:54
  7.2 4.6 copy-start
  7.2 4.6 copy-start.1
  10.8 441.0 %reduce-scatter.2.cloned.1.call-start = ((), (), s32[]{:S(2)}) async-start(), calls=%async_computation.2 | async-start | bytes 37748736 | tf_op jit(solution)/shard_map/reduce_scatter | solution.py:59
Sparse Core Ops, SparseCore 0:
  10.9 90.1 all-gather.1
  126.3 325.4 reduce-scatter.1
where the time goes:
time: 466 us; the launch traced here: 465 us
  waiting for transfers between devices  385 us (83%)
  matrix products  51.6 us (11%)
  between operations  14.9 us (3%)
  other arithmetic  13.3 us (3%)
    reduce_scatter x1, waiting for transfers between devices, on_device(): lax.psum_scatter((running * dequant).astype(jnp.bfloat16), 'dp', scatter_...  326 us
    all_gather x1, waiting for transfers between devices, on_device(): lax.all_gather(grad_scaled, 'tensor', axis=0, tiled=True)  58.9 us
    dot_general x1, matrix products, on_device(): lax.dot_general(lax.all_gather(grad_scaled, 'tensor', axis=0, tiled=True)...  25 us
    dot_general x16, matrix products, attend(): jnp.dot(query_rows, key_rows.T, preferred_element_type=jnp.float32)  19.7 us
  transfers between devices with their start and end apart: 2, of which 2 were waited for; matrix products, arithmetic and copies ran while one was open for 6% of the time, Pallas kernels for 0%

commit v1 on v0

v1 whole, which is shorter than its diff:
```python
import functools

import jax
import jax.numpy as jnp
from jax import lax
from jax.experimental import pallas as pl
from jax.experimental.pallas import tpu as pltpu
from jax.sharding import PartitionSpec as P

HEAD_DIM = 128
SATURATION = 448.0
CHUNKS = 4


def quantize(values_in, exponent):
    factor = SATURATION * jnp.exp2(-exponent[0].astype(jnp.float32))
    return jnp.clip(values_in * factor, -SATURATION, SATURATION).astype(jnp.bfloat16)


def attend_group(queries, key_rows, value_rows):
    seq_len = queries.shape[0]
    heads = queries.shape[1] // HEAD_DIM
    stacked = queries.reshape(seq_len, heads, HEAD_DIM)
    scores = jnp.einsum(
        "thd,ud->htu", stacked, key_rows, preferred_element_type=jnp.float32
    ) * HEAD_DIM ** (-0.5)
    positions = jnp.arange(seq_len, dtype=jnp.int32)
    causal = positions[None, :] <= positions[:, None]
    scores = jnp.where(causal[None], scores, jnp.float32(-1e30))
    row_max = jnp.max(scores, axis=2, keepdims=True)
    weights = jnp.exp(scores - row_max)
    probabilities = (weights / jnp.sum(weights, axis=2, keepdims=True)).astype(jnp.bfloat16)
    out = jnp.einsum(
        "htu,ud->thd", probabilities, value_rows, preferred_element_type=jnp.float32
    )
    return out.reshape(seq_len, heads * HEAD_DIM)


def gather_kernel(
    n_dp, n_t, act_ref, grad_ref, act_out, grad_out,
    a_send, a_recv, b_send, b_recv, c_send, c_recv, p_send, p_recv, own_sem,
):
    dp = lax.axis_index("dp")
    t = lax.axis_index("tensor")
    core = dp % 2
    z = dp // 2
    n_z = n_dp // 2
    partner = dp + 1 - 2 * core
    rows = act_ref.shape[0] // CHUNKS

    barrier = pltpu.get_barrier_semaphore()
    for k in range(1, n_dp):
        pl.semaphore_signal(
            barrier, inc=1, device_id={"dp": (dp + k) % n_dp, "tensor": t},
            device_id_type=pl.DeviceIdType.MESH,
        )
    for j in range(1, n_t):
        pl.semaphore_signal(
            barrier, inc=1, device_id={"dp": dp, "tensor": (t + j) % n_t},
            device_id_type=pl.DeviceIdType.MESH,
        )
    pl.semaphore_wait(barrier, n_dp + n_t - 2)

    def remote(src, dst, send, recv, to_dp, to_t):
        return pltpu.make_async_remote_copy(
            src_ref=src, dst_ref=dst, send_sem=send, recv_sem=recv,
            device_id={"dp": to_dp, "tensor": to_t}, device_id_type=pl.DeviceIdType.MESH,
        )

    def stage_a(k):
        to = (dp + k) % n_dp
        return remote(
            grad_ref.at[to], grad_out.at[dp, t], a_send.at[k], a_recv.at[k], to, t
        )

    def stage_b(k, j):
        owner = (dp + n_dp - k) % n_dp
        src = grad_ref.at[dp] if k == 0 else grad_out.at[owner, t]
        return remote(
            src, grad_out.at[owner, t], b_send.at[k, j], b_recv.at[k, j], dp, (t + j) % n_t
        )

    def part(block, q):
        return act_out.at[block, pl.ds(q * rows, rows)]

    def chain(side, i, q):
        step = 1 - 2 * side
        block = (z - i * step) * 2 + core
        src = act_ref.at[pl.ds(q * rows, rows)] if i == 0 else part(block, q)
        return remote(
            src, part(block, q), c_send.at[side, i, q], c_recv.at[side, i, q],
            dp + 2 * step, t,
        )

    def can_send(side, i):
        if side == 0:
            return (z - i >= 0) & (z + 1 < n_z)
        return (z + i < n_z) & (z - 1 >= 0)

    def can_take(side, i):
        return z - 1 - i >= 0 if side == 0 else z + 1 + i < n_z

    def share(side, i, q):
        step = 1 - 2 * side
        block = (z - (i + 1) * step) * 2 + core
        return remote(
            part(block, q), part(block, q), p_send.at[side, i, q], p_recv.at[side, i, q],
            partner, t,
        )

    def share_own(q):
        return remote(
            act_ref.at[pl.ds(q * rows, rows)], part(dp, q),
            p_send.at[0, n_z - 1, q], p_recv.at[0, n_z - 1, q], partner, t,
        )

    for k in range(1, n_dp):
        stage_a(k).start()
    for q in range(CHUNKS):
        for side in range(2):
            @pl.when(can_send(side, 0))
            def _():
                chain(side, 0, q).start()
    for j in range(1, n_t):
        stage_b(0, j).start()
    for q in range(CHUNKS):
        share_own(q).start()
    own_act = pltpu.make_async_copy(act_ref, act_out.at[dp], own_sem.at[0])
    own_grad = pltpu.make_async_copy(grad_ref.at[dp], grad_out.at[dp, t], own_sem.at[1])
    own_act.start()
    own_grad.start()
    for k in range(1, n_dp):
        stage_a(k).wait_recv()
        for j in range(1, n_t):
            stage_b(k, j).start()
    for i in range(n_z - 1):
        for q in range(CHUNKS):
            for side in range(2):
                @pl.when(can_take(side, i))
                def _():
                    chain(side, i, q).wait_recv()
                    if i + 1 < n_z - 1:
                        @pl.when(can_send(side, i + 1))
                        def _():
                            chain(side, i + 1, q).start()
                    share(side, i, q).start()
    own_act.wait()
    own_grad.wait()
    for q in range(CHUNKS):
        share_own(q).wait()
    for k in range(1, n_dp):
        stage_a(k).wait_send()
    for k in range(n_dp):
        for j in range(1, n_t):
            stage_b(k, j).wait()
    for i in range(n_z - 1):
        for q in range(CHUNKS):
            for side in range(2):
                @pl.when(can_send(side, i))
                def _():
                    chain(side, i, q).wait_send()

                @pl.when(can_take(side, i))
                def _():
                    share(side, i, q).wait()


def gather_all(act, grad_blocks, n_t):
    n_dp, rows, cols = grad_blocks.shape
    n_z = n_dp // 2
    dma = pltpu.SemaphoreType.DMA
    return pl.pallas_call(
        functools.partial(gather_kernel, n_dp, n_t),
        out_shape=(
            jax.ShapeDtypeStruct((n_dp,) + act.shape, act.dtype),
            jax.ShapeDtypeStruct((n_dp, n_t, rows, cols), act.dtype),
        ),
        in_specs=[pl.BlockSpec(memory_space=pltpu.VMEM)] * 2,
        out_specs=(pl.BlockSpec(memory_space=pl.ANY),) * 2,
        scratch_shapes=[
            dma((n_dp,)), dma((n_dp,)),
            dma((n_dp, n_t)), dma((n_dp, n_t)),
            dma((2, n_z, CHUNKS)), dma((2, n_z, CHUNKS)),
            dma((2, n_z, CHUNKS)), dma((2, n_z, CHUNKS)),
            dma((2,)),
        ],
        compiler_params=pltpu.CompilerParams(
            collective_id=0, has_side_effects=True, vmem_limit_bytes=60 * 1024 * 1024
        ),
    )(act, grad_blocks)


def on_device(n_dp, n_t, saved_queries, saved_keys, saved_values, out_grad, act_exponent, grad_exponent):
    groups = saved_keys.shape[1] // HEAD_DIM
    width = saved_queries.shape[1] // groups
    dequant = jnp.exp2((act_exponent[0] + grad_exponent[0]).astype(jnp.float32)) / (
        SATURATION * SATURATION
    )
    rows, d_model = out_grad.shape
    cols = d_model // n_dp
    grad_scaled = quantize(out_grad.astype(jnp.float32), grad_exponent)
    grad_blocks = grad_scaled.reshape(rows, n_dp, cols).transpose(1, 0, 2)
    acts = []
    for g in range(groups):
        k = saved_keys[:, g * HEAD_DIM:(g + 1) * HEAD_DIM]
        v = saved_values[:, g * HEAD_DIM:(g + 1) * HEAD_DIM]
        q = saved_queries[:, g * width:(g + 1) * width]
        acts.append(quantize(attend_group(q, k, v), act_exponent))
    act = jnp.concatenate(acts, axis=1)
    act_all, grad_all = gather_all(act, grad_blocks, n_t)
    act_rows = act_all.reshape(-1, act.shape[1])
    grad_rows = grad_all.reshape(-1, cols)
    return lax.dot_general(
        grad_rows, act_rows, (((0,), (0,)), ((), ())), preferred_element_type=jnp.float32
    ) * dequant


def solution(mesh):
    in_specs = (
        P("dp", "tensor"),
        P("dp", "tensor"),
        P("dp", "tensor"),
        P(("dp", "tensor"), None),
        P(),
        P(),
    )
    return jax.shard_map(
        functools.partial(on_device, mesh.shape["dp"], mesh.shape["tensor"]),
        mesh=mesh,
        in_specs=in_specs, out_specs=P("dp", "tensor"), check_vma=False
    )
```

time: 466 us -> 245 us (0.53)
  waiting for transfers between devices: 385 us -> 0 us
  Pallas kernels: 0 us -> 181 us
  between operations: 14.9 us -> 1.52 us
  local copies, waits for them, and re-layouts: 0.25 us -> 10.6 us
  other arithmetic: 13.3 us -> 3.72 us
    reduce_scatter x1 -> x0, waiting for transfers between devices: 326 us -> none  [on_device(): lax.psum_scatter((running * dequant).astype(jnp.bfloat16), 'dp', scatter_...]
    pallas_call x0 -> x1, Pallas kernels: none -> 181 us  [gather_all(): pl.pallas_call(functools.partial(gather_kernel, n_dp, n_t), out_shape=(ja...]
    all_gather x1 -> x0, waiting for transfers between devices: 58.9 us -> none  [on_device(): lax.all_gather(grad_scaled, 'tensor', axis=0, tiled=True)]
    dot_general x33 -> x3, matrix products: 51.6 us -> 33.1 us  [the longest x1 24.3 us: on_device(): lax.dot_general(grad_rows, act_rows, (((0,), (0,)), ((), ())), preferred_...]
    sub x0 -> x2, matrix products: none -> 14.9 us  [attend_group(): weights = jnp.exp(scores - row_max)]
    convert_element_type x1 -> x0, other arithmetic: 6.65 us -> none  [on_device(): grad_weight = lax.psum_scatter((running * dequant).astype(jnp.bfloat16),...]
    unnamed x4 -> x7, local copies, waits for them, and re-layouts: 0.01 us -> 5.17 us
  transfers between devices with their start and end apart: 2 -> 0, of which waited for: 2 -> 0; matrix products, arithmetic and copies ran while one was open for 6% -> 0% of each run, Pallas kernels for 0% -> 0%
where the time goes in v1:
time: 245 us
  Pallas kernels  181 us (74%)
  matrix products  48 us (20%)
  local copies, waits for them, and re-layouts  10.6 us (4%)
  other arithmetic  3.72 us (2%)
    pallas_call x1, Pallas kernels, gather_all(): pl.pallas_call(functools.partial(gather_kernel, n_dp, n_t), out_shape=(ja...  181 us
    dot_general x1, matrix products, on_device(): lax.dot_general(grad_rows, act_rows, (((0,), (0,)), ((), ())), preferred_...  24.3 us
    sub x2, matrix products, attend_group(): weights = jnp.exp(scores - row_max)  14.9 us
    dot_general x2, matrix products, attend_group(): jnp.einsum('htu,ud->thd', probabilities, value_rows, preferred_element_ty...  8.79 us
    unnamed x7, local copies, waits for them, and re-layouts  5.17 us

profile of v1, /device:TPU:0, one launch (start us, length us, event | category | flops | bytes accessed | tf_op | source)
XLA Modules:
  0.0 245.1 jit_solution(13784095269506294831)
XLA Ops:
  1.4 0.1 iota_compare_fusion
  1.5 4.1 %copy.23 = bf16[128,8192]{0,1:T(8,128)(2,1)} copy(bf16[128,8192]{1,0:T(8,128)(2,1)} %param.9) | data formatting | bytes 4194304 | tf_op args[3]
  5.6 2.1 clamp_convert_fusion
  7.7 2.7 %copy.24 = bf16[128,8,1024]{2,0,1:T(8,128)(2,1)} copy(bf16[128,8,1024]{0,2,1:T(8,128)(2,1)S(1)} %bitcast.78) | data formatting | bytes 4194304 | tf_op jit(solution)/shard_map/reshape | solution.py:202
  10.4 1.7 fusion.46
  12.1 0.5 copy.32
  12.6 0.5 copy.34
  13.2 0.0 copy-start
  13.2 7.5 %fusion.47 = (f32[8,512]{1,0:T(8,128)S(1)}, f32[8,512,512]{1,2,0:T(8,128)}) fusion(pred[512,512]{0,1:T(8,128)(4,1)S(1)} %iota_compare_fusion, bf16[512,8,128]{0,2,1:T(8,128)(2,1)S(1)} %bitcast.80, bf16[512,256]{1,0:T(8,128)(2,1)} %param.7), kind=kOutput, calls=%fused_computation.45 | convolution fusion | flops 545260032 | bytes 9846784 | tf_op jit(solution)/shard_map/sub | solution.py:31
  20.7 0.0 copy-done
  20.7 4.4 %clamp_convert_fusion.1 = bf16[8,512,128]{1,2,0:T(8,128)(2,1)S(1)} fusion(f32[8,512,512]{1,2,0:T(8,128)} %get-tuple-element.12, f32[8,512]{1,0:T(8,128)S(1)} %get-tuple-element.11, f32[]{:T(128)} %bitcast.4, bf16[512,256]{1,0:T(8,128)(2,1)S(1)} %copy-done), kind=kOutput, calls=%fused_computation.21 | convolution fusion | flops 542638080 | bytes 9584644 | tf_op jit(solution)/shard_map/htu,ud->thd/dot_general | solution.py:33
  25.1 0.5 copy.30
  25.6 0.0 copy-start.1
  25.6 7.5 %fusion.52 = (f32[8,512]{1,0:T(8,128)S(1)}, f32[8,512,512]{1,2,0:T(8,128)}) fusion(pred[512,512]{0,1:T(8,128)(4,1)S(1)} %iota_compare_fusion, bf16[512,8,128]{0,2,1:T(8,128)(2,1)S(1)} %bitcast.79, bf16[512,256]{1,0:T(8,128)(2,1)} %param.7), kind=kOutput, calls=%fused_computation.46 | convolution fusion | flops 545260032 | bytes 9846784 | tf_op jit(solution)/shard_map/sub | solution.py:31
  33.1 0.0 copy-done.1
  33.1 4.4 %clamp_convert_fusion.2 = bf16[8,512,128]{1,2,0:T(8,128)(2,1)S(1)} fusion(f32[8,512,512]{1,2,0:T(8,128)} %get-tuple-element.14, f32[8,512]{1,0:T(8,128)S(1)} %get-tuple-element.13, f32[]{:T(128)} %bitcast.4, bf16[512,256]{1,0:T(8,128)(2,1)S(1)} %copy-done.1), kind=kOutput, calls=%fused_computation.22 | convolution fusion | flops 542638080 | bytes 9584644 | tf_op jit(solution)/shard_map/htu,ud->thd/dot_general | solution.py:33
  37.5 0.5 copy.29
  38.0 1.5 pad_maximum_fusion.act_ref
  39.6 181.2 %shard_map.64 = (bf16[8,512,2048]{2,1,0:T(8,128)(2,1)}, bf16[8,4,128,1024]{3,2,1,0:T(8,128)(2,1)}) custom-call(bf16[512,2048]{1,0:T(8,128)(2,1)} %pad_maximum_fusion.act_ref, bf16[8,128,1024]{2,1,0:T(8,128)(2,1)} %bitcast.77), custom_call_target="tpu_custom_call" | custom-call | tf_op jit(solution)/shard_map/pallas_call | solution.py:172
  220.8 24.3 %convolution_multiply_fusion = f32[1024,2048]{1,0:T(8,128)} fusion(bf16[4096,1024]{1,0:T(8,128)(2,1)} %bitcast.84, bf16[4096,2048]{1,0:T(8,128)(2,1)} %bitcast.83, f32[]{:T(128)} %bitcast.18), kind=kOutput, calls=%fused_computation.10 | convolution fusion | flops 17181966336 | bytes 33554436 | tf_op jit(solution)/shard_map/dot_general | solution.py:213
Async XLA Ops:
  13.2 7.5 %copy-start = (bf16[512,256]{1,0:T(8,128)(2,1)S(1)}, bf16[512,256]{1,0:T(8,128)(2,1)}, u32[]{:S(2)}) copy-start(bf16[512,256]{1,0:T(8,128)(2,1)} %param.8) | copy-start | bytes 786436
  25.6 7.5 %copy-start.1 = (bf16[512,256]{1,0:T(8,128)(2,1)S(1)}, bf16[512,256]{1,0:T(8,128)(2,1)}, u32[]{:S(2)}) copy-start(bf16[512,256]{1,0:T(8,128)(2,1)} %param.8) | copy-start | bytes 786436

commit v2 on v1

--- a/solution.py
+++ b/solution.py
@@ -9,7 +9,7 @@
 
 HEAD_DIM = 128
 SATURATION = 448.0
-CHUNKS = 4
+CHUNKS = 2
 
 
 def quantize(values_in, exponent):
@@ -37,16 +37,20 @@
 
 
 def gather_kernel(
-    n_dp, n_t, act_ref, grad_ref, act_out, grad_out,
-    a_send, a_recv, b_send, b_recv, c_send, c_recv, p_send, p_recv, own_sem,
+    n_dp, n_t, groups, *refs
 ):
+    act_refs, grad_refs = refs[:groups], refs[groups:groups + n_dp]
+    act_out, grad_out = refs[groups + n_dp:groups + n_dp + 2]
+    b_send, b_recv, c_send, c_recv, p_send, p_recv, own_sem = refs[groups + n_dp + 2:]
+    chunks = CHUNKS * groups
     dp = lax.axis_index("dp")
     t = lax.axis_index("tensor")
     core = dp % 2
     z = dp // 2
     n_z = n_dp // 2
     partner = dp + 1 - 2 * core
-    rows = act_ref.shape[0] // CHUNKS
+    rows = act_refs[0].shape[0] // CHUNKS
+    width = act_refs[0].shape[1]
 
     barrier = pltpu.get_barrier_semaphore()
     for k in range(1, n_dp):
@@ -67,26 +71,24 @@
             device_id={"dp": to_dp, "tensor": to_t}, device_id_type=pl.DeviceIdType.MESH,
         )
 
-    def stage_a(k):
-        to = (dp + k) % n_dp
-        return remote(
-            grad_ref.at[to], grad_out.at[dp, t], a_send.at[k], a_recv.at[k], to, t
-        )
-
     def stage_b(k, j):
         owner = (dp + n_dp - k) % n_dp
-        src = grad_ref.at[dp] if k == 0 else grad_out.at[owner, t]
-        return remote(
-            src, grad_out.at[owner, t], b_send.at[k, j], b_recv.at[k, j], dp, (t + j) % n_t
+        return remote(
+            grad_refs[k], grad_out.at[owner, t], b_send.at[k, j], b_recv.at[k, j], dp, (t + j) % n_t
         )
 
     def part(block, q):
-        return act_out.at[block, pl.ds(q * rows, rows)]
+        return act_out.at[
+            block, pl.ds(q % CHUNKS * rows, rows), pl.ds(q // CHUNKS * width, width)
+        ]
+
+    def own_part(q):
+        return act_refs[q // CHUNKS].at[pl.ds(q % CHUNKS * rows, rows)]
 
     def chain(side, i, q):
         step = 1 - 2 * side
         block = (z - i * step) * 2 + core
-        src = act_ref.at[pl.ds(q * rows, rows)] if i == 0 else part(block, q)
+        src = own_part(q) if i == 0 else part(block, q)
         return remote(
             src, part(block, q), c_send.at[side, i, q], c_recv.at[side, i, q],
             dp + 2 * step, t,
@@ -110,31 +112,36 @@
 
     def share_own(q):
         return remote(
-            act_ref.at[pl.ds(q * rows, rows)], part(dp, q),
+            own_part(q), part(dp, q),
             p_send.at[0, n_z - 1, q], p_recv.at[0, n_z - 1, q], partner, t,
         )
 
-    for k in range(1, n_dp):
-        stage_a(k).start()
-    for q in range(CHUNKS):
+    for q in range(chunks):
         for side in range(2):
             @pl.when(can_send(side, 0))
             def _():
                 chain(side, 0, q).start()
-    for j in range(1, n_t):
-        stage_b(0, j).start()
-    for q in range(CHUNKS):
-        share_own(q).start()
-    own_act = pltpu.make_async_copy(act_ref, act_out.at[dp], own_sem.at[0])
-    own_grad = pltpu.make_async_copy(grad_ref.at[dp], grad_out.at[dp, t], own_sem.at[1])
-    own_act.start()
-    own_grad.start()
-    for k in range(1, n_dp):
-        stage_a(k).wait_recv()
+    for k in range(n_dp):
         for j in range(1, n_t):
             stage_b(k, j).start()
+    for q in range(chunks):
+        share_own(q).start()
+
+    def own_act(q):
+        return pltpu.make_async_copy(own_part(q), part(dp, q), own_sem.at[n_dp + q])
+
+    for q in range(chunks):
+        own_act(q).start()
+
+    def own_grad(k):
+        return pltpu.make_async_copy(
+            grad_refs[k], grad_out.at[(dp + n_dp - k) % n_dp, t], own_sem.at[k]
+        )
+
+    for k in range(n_dp):
+        own_grad(k).start()
     for i in range(n_z - 1):
-        for q in range(CHUNKS):
+        for q in range(chunks):
             for side in range(2):
                 @pl.when(can_take(side, i))
                 def _():
@@ -144,17 +151,17 @@
                         def _():
                             chain(side, i + 1, q).start()
                     share(side, i, q).start()
-    own_act.wait()
-    own_grad.wait()
-    for q in range(CHUNKS):
+    for q in range(chunks):
+        own_act(q).wait()
+    for k in range(n_dp):
+        own_grad(k).wait()
+    for q in range(chunks):
         share_own(q).wait()
-    for k in range(1, n_dp):
-        stage_a(k).wait_send()
     for k in range(n_dp):
         for j in range(1, n_t):
             stage_b(k, j).wait()
     for i in range(n_z - 1):
-        for q in range(CHUNKS):
+        for q in range(chunks):
             for side in range(2):
                 @pl.when(can_send(side, i))
                 def _():
@@ -165,29 +172,31 @@
                     share(side, i, q).wait()
 
 
-def gather_all(act, grad_blocks, n_t):
-    n_dp, rows, cols = grad_blocks.shape
-    n_z = n_dp // 2
+def gather_all(acts, grad_blocks, n_t):
+    n_dp, groups = len(grad_blocks), len(acts)
+    rows, cols = grad_blocks[0].shape
+    seq_len, width = acts[0].shape
+    n_z, chunks = n_dp // 2, CHUNKS * groups
+    dtype = acts[0].dtype
     dma = pltpu.SemaphoreType.DMA
     return pl.pallas_call(
-        functools.partial(gather_kernel, n_dp, n_t),
+        functools.partial(gather_kernel, n_dp, n_t, groups),
         out_shape=(
-            jax.ShapeDtypeStruct((n_dp,) + act.shape, act.dtype),
-            jax.ShapeDtypeStruct((n_dp, n_t, rows, cols), act.dtype),
+            jax.ShapeDtypeStruct((n_dp, seq_len, groups * width), dtype),
+            jax.ShapeDtypeStruct((n_dp, n_t, rows, cols), dtype),
         ),
-        in_specs=[pl.BlockSpec(memory_space=pltpu.VMEM)] * 2,
+        in_specs=[pl.BlockSpec(memory_space=pltpu.VMEM)] * (groups + n_dp),
         out_specs=(pl.BlockSpec(memory_space=pl.ANY),) * 2,
         scratch_shapes=[
-            dma((n_dp,)), dma((n_dp,)),
             dma((n_dp, n_t)), dma((n_dp, n_t)),
-            dma((2, n_z, CHUNKS)), dma((2, n_z, CHUNKS)),
-            dma((2, n_z, CHUNKS)), dma((2, n_z, CHUNKS)),
-            dma((2,)),
+            dma((2, n_z, chunks)), dma((2, n_z, chunks)),
+            dma((2, n_z, chunks)), dma((2, n_z, chunks)),
+            dma((n_dp + chunks,)),
         ],
         compiler_params=pltpu.CompilerParams(
             collective_id=0, has_side_effects=True, vmem_limit_bytes=60 * 1024 * 1024
         ),
-    )(act, grad_blocks)
+    )(*acts, *grad_blocks)
 
 
 def on_device(n_dp, n_t, saved_queries, saved_keys, saved_values, out_grad, act_exponent, grad_exponent):
@@ -199,16 +208,22 @@
     rows, d_model = out_grad.shape
     cols = d_model // n_dp
     grad_scaled = quantize(out_grad.astype(jnp.float32), grad_exponent)
-    grad_blocks = grad_scaled.reshape(rows, n_dp, cols).transpose(1, 0, 2)
+    dp = lax.axis_index("dp")
+    blocks = []
+    for k in range(n_dp):
+        to = (dp + k) % n_dp
+        block = lax.dynamic_slice_in_dim(grad_scaled, to * cols, cols, 1)
+        if k > 0:
+            block = lax.ppermute(block, "dp", [(d, (d + k) % n_dp) for d in range(n_dp)])
+        blocks.append(block)
     acts = []
     for g in range(groups):
         k = saved_keys[:, g * HEAD_DIM:(g + 1) * HEAD_DIM]
         v = saved_values[:, g * HEAD_DIM:(g + 1) * HEAD_DIM]
         q = saved_queries[:, g * width:(g + 1) * width]
         acts.append(quantize(attend_group(q, k, v), act_exponent))
-    act = jnp.concatenate(acts, axis=1)
-    act_all, grad_all = gather_all(act, grad_blocks, n_t)
-    act_rows = act_all.reshape(-1, act.shape[1])
+    act_all, grad_all = gather_all(acts, blocks, n_t)
+    act_rows = act_all.reshape(-1, act_all.shape[2])
     grad_rows = grad_all.reshape(-1, cols)
     return lax.dot_general(
         grad_rows, act_rows, (((0,), (0,)), ((), ())), preferred_element_type=jnp.float32

time: 245 us -> 226 us (0.922)
  Pallas kernels: 181 us -> 146 us
  waiting for transfers between devices: 0 us -> 14.5 us
  starting transfers between devices: 0 us -> 9.31 us
  local copies, waits for them, and re-layouts: 10.6 us -> 5.98 us
    pallas_call x1, Pallas kernels: 181 us -> 146 us  [gather_all(): pl.pallas_call(functools.partial(gather_kernel, n_dp, n_t, groups), out_s...]
    ppermute x0 -> x7, waiting for transfers between devices: none -> 14.5 us  [on_device(): lax.ppermute(block, 'dp', [(d, (d + k) % n_dp) for d in range(n_dp)])]
    ppermute x0 -> x7, starting transfers between devices: none -> 9.31 us  [on_device(): lax.ppermute(block, 'dp', [(d, (d + k) % n_dp) for d in range(n_dp)])]
    unnamed x7 -> x12, local copies, waits for them, and re-layouts: 5.17 us -> 1.88 us
    reshape x1 -> x0, local copies, waits for them, and re-layouts: 2.65 us -> none  [on_device(): grad_blocks = grad_scaled.reshape(rows, n_dp, cols).transpose(1, 0, 2)]
  transfers between devices with their start and end apart: 0 -> 7, of which waited for: 0 -> 1; matrix products, arithmetic and copies ran while one was open for 0% -> 12% of each run, Pallas kernels for 0% -> 0%
where the time goes in v2:
time: 226 us
  Pallas kernels  146 us (65%)
  matrix products  45.7 us (20%)
  waiting for transfers between devices  14.5 us (6%)
  starting transfers between devices  9.31 us (4%)
  local copies, waits for them, and re-layouts  5.98 us (3%)
  other arithmetic  3.04 us (1%)
    pallas_call x1, Pallas kernels, gather_all(): pl.pallas_call(functools.partial(gather_kernel, n_dp, n_t, groups), out_s...  146 us
    dot_general x1, matrix products, on_device(): lax.dot_general(grad_rows, act_rows, (((0,), (0,)), ((), ())), preferred_...  24.2 us
    ppermute x7, waiting for transfers between devices, on_device(): lax.ppermute(block, 'dp', [(d, (d + k) % n_dp) for d in range(n_dp)])  14.5 us
    sub x2, matrix products, attend_group(): weights = jnp.exp(scores - row_max)  12.6 us
    ppermute x7, starting transfers between devices, on_device(): lax.ppermute(block, 'dp', [(d, (d + k) % n_dp) for d in range(n_dp)])  9.31 us
    dot_general x2, matrix products, attend_group(): jnp.einsum('htu,ud->thd', probabilities, value_rows, preferred_element_ty...  8.96 us
  transfers between devices with their start and end apart: 7, of which 1 were waited for; matrix products, arithmetic and copies ran while one was open for 12% of the time, Pallas kernels for 0%

profile of v2, /device:TPU:0, one launch (start us, length us, event | category | flops | bytes accessed | tf_op | source)
XLA Modules:
  0.0 225.7 jit_solution(8746290869378458756)
XLA Ops:
  0.7 0.0 copy-start
  0.7 2.3 %clamp_convert_fusion = bf16[128,8192]{1,0:T(8,128)(2,1)S(1)} fusion(bf16[128,8192]{1,0:T(8,128)(2,1)} %param.9, f32[]{:T(128)} %bitcast.13), kind=kLoop, calls=%fused_computation.11 | loop fusion | flops 4194304 | bytes 4194308 | tf_op jit(solution)/shard_map/convert_element_type | solution.py:17
  3.0 1.3 constant_dynamic-slice_fusion
  4.3 4.5 %collective-permute-start.6 = (bf16[128,1024]{1,0:T(8,128)(2,1)}, bf16[128,1024]{1,0:T(8,128)(2,1)}, u32[]{:S(2)}, u32[]{:S(2)}) collective-permute-start(bf16[128,1024]{1,0:T(8,128)(2,1)} %get-tuple-element.9), channel_id=1, source_target_pairs={{0,28},{4,0},{8,4},{12,8},{16,12},{20,16},{24,20},{28,24},{1,29},{... | collective-permute-start | bytes 786440 | tf_op jit(solution)/shard_map/ppermute | solution.py:217
  8.8 0.6 collective-permute-start.5
  9.3 0.0 collective-permute-start.4
  9.4 2.8 %collective-permute-start.3 = (bf16[128,1024]{1,0:T(8,128)(2,1)}, bf16[128,1024]{1,0:T(8,128)(2,1)}, u32[]{:S(2)}, u32[]{:S(2)}) collective-permute-start(bf16[128,1024]{1,0:T(8,128)(2,1)} %get-tuple-element.12), channel_id=1, source_target_pairs={{0,16},{4,20},{8,24},{12,28},{16,0},{20,4},{24,8},{28,12},{1,17},{... | collective-permute-start | bytes 786440 | tf_op jit(solution)/shard_map/ppermute | solution.py:217
  12.1 0.0 collective-permute-start.2
  12.1 0.8 iota_compare_fusion
  13.6 0.0 copy-done
  13.6 0.2 fusion.46
  13.8 0.5 copy.32
  14.3 0.5 copy.30
  14.9 7.6 %fusion.47 = (f32[8,512]{1,0:T(8,128)S(1)}, f32[8,512,512]{1,2,0:T(8,128)}) fusion(pred[512,512]{0,1:T(8,128)(4,1)} %iota_compare_fusion, bf16[512,8,128]{0,2,1:T(8,128)(2,1)S(1)} %bitcast.78, bf16[512,256]{1,0:T(8,128)(2,1)} %param.7), kind=kOutput, calls=%fused_computation.52 | convolution fusion | flops 545260032 | bytes 9846784 | tf_op jit(solution)/shard_map/sub | solution.py:31
  22.4 0.0 copy-start.3
  22.4 0.0 copy-start.4
  22.4 4.5 %clamp_convert_fusion.2 = bf16[8,512,128]{1,2,0:T(8,128)(2,1)S(1)} fusion(f32[8,512,512]{1,2,0:T(8,128)} %get-tuple-element.20, f32[8,512]{1,0:T(8,128)S(1)} %get-tuple-element.19, f32[]{:T(128)} %bitcast.4, bf16[512,256]{1,0:T(8,128)(2,1)} %param.8), kind=kOutput, calls=%fused_computation.21 | convolution fusion | flops 542638080 | bytes 9585152 | tf_op jit(solution)/shard_map/htu,ud->thd/dot_general | solution.py:33
  26.9 0.0 copy-done.3
  27.0 0.0 copy-done.4
  27.0 5.0 %fusion.52 = (f32[8,512]{1,0:T(8,128)S(1)}, f32[8,512,512]{1,2,0:T(8,128)}) fusion(pred[512,512]{0,1:T(8,128)(4,1)S(1)} %copy-done.3, bf16[512,8,128]{0,2,1:T(8,128)(2,1)S(1)} %bitcast.76, bf16[512,256]{1,0:T(8,128)(2,1)S(1)} %copy-done.4), kind=kOutput, calls=%fused_computation.53 | convolution fusion | flops 545260032 | bytes 9846784 | tf_op jit(solution)/shard_map/sub | solution.py:31
  32.0 0.0 collective-permute-done.6.refs_9_
  32.0 0.6 collective-permute-start.1
  32.6 0.0 collective-permute-done.5.refs_8_
  32.6 0.8 collective-permute-start
  33.5 4.5 %clamp_convert_fusion.1 = bf16[8,512,128]{1,2,0:T(8,128)(2,1)S(1)} fusion(f32[8,512,512]{1,2,0:T(8,128)} %get-tuple-element.22, f32[8,512]{1,0:T(8,128)S(1)} %get-tuple-element.21, f32[]{:T(128)} %bitcast.4, bf16[512,256]{1,0:T(8,128)(2,1)} %param.8), kind=kOutput, calls=%fused_computation.20 | convolution fusion | flops 542638080 | bytes 9585152 | tf_op jit(solution)/shard_map/htu,ud->thd/dot_general | solution.py:33
  38.0 1.3 copy.27.refs_0_
  39.3 1.3 copy.28.refs_1_
  40.7 0.0 collective-permute-done.4.refs_7_
  40.7 14.5 %collective-permute-done.3.refs_6_ = bf16[128,1024]{1,0:T(8,128)(2,1)} collective-permute-done((bf16[128,1024]{1,0:T(8,128)(2,1)}, bf16[128,1024]{1,0:T(8,128)(2,1)}, u32[]{:S(2)}, u32[]{:S(2)}) %collective-permute-start.3) | collective-permute-done | bytes 262176 | tf_op jit(solution)/shard_map/ppermute | solution.py:217
  55.1 0.0 collective-permute-done.2.refs_5_
  55.1 0.0 collective-permute-done.1.refs_4_
  55.1 0.0 copy-start.1
  55.1 0.0 collective-permute-done.refs_3_
  55.1 0.0 copy-start.2
  55.1 0.7 copy-done.1
  55.8 0.1 copy-done.2
  55.9 145.7 %shard_map.64 = (bf16[8,512,2048]{2,1,0:T(8,128)(2,1)}, bf16[8,4,128,1024]{3,2,1,0:T(8,128)(2,1)}) custom-call(bf16[512,1024]{1,0:T(8,128)(2,1)} %copy.27.refs_0_, bf16[512,1024]{1,0:T(8,128)(2,1)} %copy.28.refs_1_, bf16[128,1024]{1,0:T(8,128)(2,1)} %get-tuple-element.16.refs_2_, bf16[128,1024]{1,0:T(8,128)(2,1)} %copy-done.2, bf16[128,1024]{1,0:T(8,128)(2,1)} %copy-done.1, ...), custom_call_target="tpu_custom_call" | custom-call | tf_op jit(solution)/shard_map/pallas_call | solution.py:182
  201.6 24.2 %convolution_multiply_fusion = f32[1024,2048]{1,0:T(8,128)} fusion(bf16[4096,1024]{1,0:T(8,128)(2,1)} %bitcast.80, bf16[4096,2048]{1,0:T(8,128)(2,1)} %bitcast.79, f32[]{:T(128)} %bitcast.16), kind=kOutput, calls=%fused_computation.10 | convolution fusion | flops 17181966336 | bytes 33554436 | tf_op jit(solution)/shard_map/dot_general | solution.py:228
Async XLA Ops:
  0.7 12.9 %copy-start = (bf16[512,2048]{1,0:T(8,128)(2,1)S(1)}, bf16[512,2048]{1,0:T(8,128)(2,1)}, u32[]{:S(2)}) copy-start(bf16[512,2048]{1,0:T(8,128)(2,1)} %param.6) | copy-start | bytes 6291460
  4.3 27.7 %collective-permute-start.6 = (bf16[128,1024]{1,0:T(8,128)(2,1)}, bf16[128,1024]{1,0:T(8,128)(2,1)}, u32[]{:S(2)}, u32[]{:S(2)}) collective-permute-start(bf16[128,1024]{1,0:T(8,128)(2,1)} %get-tuple-element.9), channel_id=1, source_target_pairs={{0,28},{4,0},{8,4},{12,8},{16,12},{20,16},{24,20},{28,24},{1,29},{... | collective-permute-start | bytes 786440 | tf_op jit(solution)/shard_map/ppermute | solution.py:217
  8.8 23.9 %collective-permute-start.5 = (bf16[128,1024]{1,0:T(8,128)(2,1)}, bf16[128,1024]{1,0:T(8,128)(2,1)}, u32[]{:S(2)}, u32[]{:S(2)}) collective-permute-start(bf16[128,1024]{1,0:T(8,128)(2,1)} %get-tuple-element.10), channel_id=1, source_target_pairs={{0,24},{4,28},{8,0},{12,4},{16,8},{20,12},{24,16},{28,20},{1,25},{... | collective-permute-start | bytes 786440 | tf_op jit(solution)/shard_map/ppermute | solution.py:217
  9.3 31.3 %collective-permute-start.4 = (bf16[128,1024]{1,0:T(8,128)(2,1)}, bf16[128,1024]{1,0:T(8,128)(2,1)}, u32[]{:S(2)}, u32[]{:S(2)}) collective-permute-start(bf16[128,1024]{1,0:T(8,128)(2,1)} %get-tuple-element.11), channel_id=1, source_target_pairs={{0,20},{4,24},{8,28},{12,0},{16,4},{20,8},{24,12},{28,16},{1,21},{... | collective-permute-start | bytes 786440 | tf_op jit(solution)/shard_map/ppermute | solution.py:217
  9.4 45.8 %collective-permute-start.3 = (bf16[128,1024]{1,0:T(8,128)(2,1)}, bf16[128,1024]{1,0:T(8,128)(2,1)}, u32[]{:S(2)}, u32[]{:S(2)}) collective-permute-start(bf16[128,1024]{1,0:T(8,128)(2,1)} %get-tuple-element.12), channel_id=1, source_target_pairs={{0,16},{4,20},{8,24},{12,28},{16,0},{20,4},{24,8},{28,12},{1,17},{... | collective-permute-start | bytes 786440 | tf_op jit(solution)/shard_map/ppermute | solution.py:217
  12.1 43.0 %collective-permute-start.2 = (bf16[128,1024]{1,0:T(8,128)(2,1)}, bf16[128,1024]{1,0:T(8,128)(2,1)}, u32[]{:S(2)}, u32[]{:S(2)}) collective-permute-start(bf16[128,1024]{1,0:T(8,128)(2,1)} %get-tuple-element.13), channel_id=1, source_target_pairs={{0,12},{4,16},{8,20},{12,24},{16,28},{20,0},{24,4},{28,8},{1,13},{... | collective-permute-start | bytes 786440 | tf_op jit(solution)/shard_map/ppermute | solution.py:217
  22.4 4.5 %copy-start.3 = (pred[512,512]{0,1:T(8,128)(4,1)S(1)}, pred[512,512]{0,1:T(8,128)(4,1)}, u32[]{:S(2)}) copy-start(pred[512,512]{0,1:T(8,128)(4,1)} %iota_compare_fusion) | copy-start | bytes 786436
  22.4 4.5 %copy-start.4 = (bf16[512,256]{1,0:T(8,128)(2,1)S(1)}, bf16[512,256]{1,0:T(8,128)(2,1)}, u32[]{:S(2)}) copy-start(bf16[512,256]{1,0:T(8,128)(2,1)} %param.7) | copy-start | bytes 786436
  32.0 23.1 %collective-permute-start.1 = (bf16[128,1024]{1,0:T(8,128)(2,1)}, bf16[128,1024]{1,0:T(8,128)(2,1)S(1)}, u32[]{:S(2)}, u32[]{:S(2)}) collective-permute-start(bf16[128,1024]{1,0:T(8,128)(2,1)} %get-tuple-element.14), channel_id=1, source_target_pairs={{0,8},{4,12},{8,16},{12,20},{16,24},{20,28},{24,0},{28,4},{1,9},{5... | collective-permute-start | bytes 786440 | tf_op jit(solution)/shard_map/ppermute | solution.py:217
  32.6 22.5 %collective-permute-start = (bf16[128,1024]{1,0:T(8,128)(2,1)S(1)}, bf16[128,1024]{1,0:T(8,128)(2,1)S(1)}, u32[]{:S(2)}, u32[]{:S(2)}) collective-permute-start(bf16[128,1024]{1,0:T(8,128)(2,1)S(1)} %get-tuple-element.15), channel_id=1, source_target_pairs={{0,4},{4,8},{8,12},{12,16},{16,20},{20,24},{24,28},{28,0},{1,5},{5... | collective-permute-start | bytes 786440 | tf_op jit(solution)/shard_map/ppermute | solution.py:217
  55.1 0.7 copy-start.1
  55.1 0.8 copy-start.2
